TPU v7x, 32 devices: a whole 2x2x4 slice. The times are simulated.
32 devices in a mesh: section: 4 (over y, core), rep: 2 (over x), tp: 4 (over z).
Axes of the slice: x: 2, y: 2, z: 4, core: 2. Of those that a mesh axis runs over, the one named last changes fastest.
Arguments:
- token_ids: int32 [2, 8, 128], P('rep', None, 'tp'), may hold values from 0 to 16383
- embed: bfloat16 [16384, 1024], P('section'), may hold values from -6 to 6
- w_in: bfloat16 [2, 4, 2, 1024, 2816], P('rep', 'section', None, None, 'tp'), may hold values from -0.1875 to 0.1875
- w_down: bfloat16 [2, 4, 2816, 1024], P('rep', 'section', 'tp'), may hold values from -0.109375 to 0.109375
- outer_in: float32 [4, 2, 1024, 2816], P('section', None, None, 'tp'), may hold values from -0.1875 to 0.1875
- outer_down: float32 [4, 2816, 1024], P('section', 'tp'), may hold values from -0.109375 to 0.109375
- moment_in: float32 [4, 2, 1024, 2816], P('section', None, None, 'tp'), may hold values from -0.12 to 0.12
- moment_down: float32 [4, 2816, 1024], P('section', 'tp'), may hold values from -0.12 to 0.12
- cotangent: bfloat16 [2, 8, 128, 1024], P('rep', None, 'tp'), may hold values from -6 to 6
- fragment: int32 [4], replicated, may hold values 0 or 1
Outputs:
- new_in: bfloat16 [2, 4, 2, 1024, 2816], P('rep', 'section', None, None, 'tp')
- new_down: bfloat16 [2, 4, 2816, 1024], P('rep', 'section', 'tp')
- next_outer_in: float32 [4, 2, 1024, 2816], P('section', None, None, 'tp')
- next_outer_down: float32 [4, 2816, 1024], P('section', 'tp')
- next_moment_in: float32 [4, 2, 1024, 2816], P('section', None, None, 'tp')
- next_moment_down: float32 [4, 2816, 1024], P('section', 'tp')
All inputs are finite; a program needn't handle non-finite values.
Results may differ from a plain program's by a relative error of at most 0.03.
Values may be sent and summed in bfloat16 or wider, within the bound.
A program may use at most 128 MiB of HBM per device.

v0:
```python
import jax
import jax.numpy as jnp
from jax import lax
from jax.sharding import PartitionSpec as P

EPS = 1e-05
INNER_LR = 0.001
OUTER_LR = 0.7
MOMENTUM = 0.9


def from_behind(value, axis, steps):
    count = lax.axis_size(axis)
    initial, last = (max(0, -steps), min(count, count - steps))
    return lax.ppermute(value, axis, [(source, source + steps) for source in range(initial, last)])


def scale_rows(values):
    return lax.rsqrt(jnp.mean(values * values, axis=-1, keepdims=True) + EPS)


def gather_rows(values):
    return lax.all_gather(values, "tp", axis=0, tiled=True)


def pass_along(values, step):
    return from_behind(values, "section", step)


def reduce_rows(left, right, form):
    return lax.psum_scatter(
        jnp.einsum(form, left, right, preferred_element_type=jnp.float32),
        "tp",
        scatter_dimension=0,
        tiled=True,
    )


def layer_forward(x_own, pair, down):
    full = gather_rows(x_own).astype(jnp.float32)
    normed = (full * scale_rows(full)).astype(jnp.bfloat16)
    gate_up = jnp.einsum("td,kdf->tkf", normed, pair, preferred_element_type=jnp.float32)
    hidden = (jax.nn.silu(gate_up[:, 0]) * gate_up[:, 1]).astype(jnp.bfloat16)
    out = reduce_rows(hidden, down, "tf,fd->td")
    return ((x_own.astype(jnp.float32) + out).astype(jnp.bfloat16), normed, gate_up)


def layer_backward(grad_own, x_own, pair, down, normed, gate_up):
    grad_full = gather_rows(grad_own)
    d_hidden = jnp.einsum("td,fd->tf", grad_full, down, preferred_element_type=jnp.float32)
    gate = gate_up[:, 0]
    upper = gate_up[:, 1]
    sig = jax.nn.sigmoid(gate)
    active = jax.nn.silu(gate)
    hidden = (active * upper).astype(jnp.bfloat16)
    d_both = jnp.stack(
        [d_hidden * upper * sig * (1.0 + gate * (1.0 - sig)), d_hidden * active], axis=1
    ).astype(jnp.bfloat16)
    g_down = jnp.einsum("tf,td->fd", hidden, grad_full, preferred_element_type=jnp.float32)
    g_pair = jnp.einsum("td,tkf->kdf", normed, d_both, preferred_element_type=jnp.float32)
    d_norm = reduce_rows(d_both, pair, "tkf,kdf->td")
    xf = x_own.astype(jnp.float32)
    rinv = scale_rows(xf)
    d_x = (
        grad_own.astype(jnp.float32)
        + rinv * d_norm
        - xf * (rinv * rinv * rinv) * jnp.mean(d_norm * xf, axis=-1, keepdims=True)
    )
    return (d_x.astype(jnp.bfloat16), g_pair, g_down)


def shards(
    token_ids,
    embed,
    w_in,
    w_down,
    outer_in,
    outer_down,
    moment_in,
    moment_down,
    cotangent,
    fragment,
):
    sections = lax.axis_size("section")
    section = lax.axis_index("section")
    replicas = lax.axis_size("rep")
    ids = token_ids[0]
    batches, own_rows = ids.shape
    vocab_part, width = embed.shape
    local_ids = ids - section * vocab_part
    inside = (local_ids >= 0) & (local_ids < vocab_part)
    looked = jnp.take(embed, jnp.clip(local_ids, 0, vocab_part - 1), axis=0).astype(jnp.float32)
    looked = jnp.where(inside[:, :, None], looked, 0.0)
    start_rows = lax.psum(looked.astype(jnp.bfloat16), "section")
    pairs = w_in[0]
    downs = w_down[0]
    depth = pairs.shape[0]
    hidden_width = pairs.shape[-1]
    total_rows = own_rows * lax.axis_size("tp")
    ticks = batches + sections - 1
    first = section == 0
    final = section == sections - 1

    def forward_tick(tick, carry):
        inbox, x_store, normed_store, gate_store = carry
        micro = tick - section
        valid = (micro >= 0) & (micro < batches)
        slot = jnp.where(valid, micro, batches)
        feed = lax.dynamic_index_in_dim(
            start_rows, jnp.clip(tick, 0, batches - 1).astype(jnp.int32), 0, keepdims=False
        )
        current = jnp.where(first, feed, inbox)
        zero = jnp.zeros((), jnp.int32)
        x_store = lax.dynamic_update_slice(
            x_store, current[None, None], (slot, zero + 0, zero, zero)
        )
        current, normed, gate_up = layer_forward(current, pairs[0], downs[0])
        normed_store = lax.dynamic_update_slice(
            normed_store, normed[None, None], (slot, zero + 0, zero, zero)
        )
        gate_store = lax.dynamic_update_slice(
            gate_store, gate_up[None, None], (slot, zero + 0, zero, zero, zero)
        )
        return (pass_along(current, 1), x_store, normed_store, gate_store)

    start_carry = (
        jnp.zeros((own_rows, width), jnp.bfloat16),
        jnp.zeros((batches + 1, depth, own_rows, width), jnp.bfloat16),
        jnp.zeros((batches + 1, depth, total_rows, width), jnp.bfloat16),
        jnp.zeros((batches + 1, depth, total_rows, 2, hidden_width), jnp.float32),
    )
    _, x_store, normed_store, gate_store = lax.fori_loop(0, ticks, forward_tick, start_carry)
    seeds = cotangent[0]

    def backward_tick(tick, carry):
        inbox, acc_pair, acc_down = carry
        micro = tick - (sections - 1 - section)
        valid = (micro >= 0) & (micro < batches)
        index = jnp.clip(micro, 0, batches - 1)
        feed = lax.dynamic_index_in_dim(seeds, index, 0, keepdims=False)
        grad = jnp.where(final, feed, inbox)
        grad = jnp.where(valid, grad, jnp.zeros_like(grad))
        zero = jnp.zeros((), jnp.int32)
        for layer in reversed(range(depth)):
            x_own = lax.dynamic_slice(
                x_store, (index, zero + layer, zero, zero), (1, 1, own_rows, width)
            )[0, 0]
            normed = lax.dynamic_slice(
                normed_store, (index, zero + layer, zero, zero), (1, 1, total_rows, width)
            )[0, 0]
            gate_up = lax.dynamic_slice(
                gate_store,
                (index, zero + layer, zero, zero, zero),
                (1, 1, total_rows, 2, hidden_width),
            )[0, 0]
            grad, g_pair, g_down = layer_backward(
                grad, x_own, pairs[layer], downs[layer], normed, gate_up
            )
            acc_pair = acc_pair.at[layer].add(g_pair)
            acc_down = acc_down.at[layer].add(g_down)
        return (pass_along(grad, -1), acc_pair, acc_down)

    back_carry = (
        jnp.zeros((own_rows, width), jnp.bfloat16),
        jnp.zeros(pairs.shape, jnp.float32),
        jnp.zeros(downs.shape, jnp.float32),
    )
    _, acc_pair, acc_down = lax.fori_loop(0, ticks, backward_tick, back_carry)
    new_pair = (pairs.astype(jnp.float32) - INNER_LR * acc_pair).astype(jnp.bfloat16)
    new_out = (downs.astype(jnp.float32) - INNER_LR * acc_down).astype(jnp.bfloat16)
    every_pair, every_down = (
        lax.all_gather(new_pair[None], "rep", axis=0, tiled=True),
        lax.all_gather(new_out[None], "rep", axis=0, tiled=True),
    )
    sum_pair = jnp.sum(every_pair.astype(jnp.float32), axis=0)
    sum_down = jnp.sum(every_down.astype(jnp.float32), axis=0)
    mean_pair = outer_in - sum_pair / replicas
    mean_down = outer_down - sum_down / replicas
    flag = lax.dynamic_index_in_dim(fragment, section, 0, keepdims=False)
    chosen = flag == 1
    moment_pair = MOMENTUM * moment_in + mean_pair
    moment_out = MOMENTUM * moment_down + mean_down
    outer_pair = outer_in - OUTER_LR * (mean_pair + MOMENTUM * moment_pair)
    outer_out = outer_down - OUTER_LR * (mean_down + MOMENTUM * moment_out)
    result_pair = jnp.where(chosen, outer_pair.astype(jnp.bfloat16), new_pair)
    result_down = jnp.where(chosen, outer_out.astype(jnp.bfloat16), new_out)
    return (
        result_pair[None],
        result_down[None],
        jnp.where(chosen, outer_pair, outer_in),
        jnp.where(chosen, outer_out, outer_down),
        jnp.where(chosen, moment_pair, moment_in),
        jnp.where(chosen, moment_out, moment_down),
    )


def solution(mesh):
    return jax.shard_map(
        shards,
        mesh=mesh,
        in_specs=(
            P("rep", None, "tp"),
            P("section", None),
            P("rep", "section", None, None, "tp"),
            P("rep", "section", "tp", None),
            P("section", None, None, "tp"),
            P("section", "tp", None),
            P("section", None, None, "tp"),
            P("section", "tp", None),
            P("rep", None, "tp", None),
            P(),
        ),
        out_specs=(
            P("rep", "section", None, None, "tp"),
            P("rep", "section", "tp", None),
            P("section", None, None, "tp"),
            P("section", "tp", None),
            P("section", None, None, "tp"),
            P("section", "tp", None),
        ),
        check_vma=False,
    )
```

profile of v0, /device:TPU:0, one launch (start us, length us, event | category | flops | bytes accessed | tf_op | source)
XLA Modules:
  0.0 1249.5 jit_solution(3856151392380230476)
XLA Ops:
  16.5 36.3 %all-reduce.2.cloned.1.call-done = bf16[8,32,1024]{2,1,0:T(8,128)(2,1)} async-done(((bf16[8,32,1024]{2,1,0:T(8,128)(2,1)}), bf16[8,32,1024]{2,1,0:T(8,128)(2,1)}) %all-reduce.2.cloned.1.call-update) | async-done | bytes 524304 | tf_op jit(solution)/shard_map/psum | solution.py:94
  58.9 500.8 %while.42 = (s32[]{:T(128)}, bf16[32,1024]{1,0:T(8,128)(2,1)S(1)}, bf16[9,1,32,1024]{3,2,1,0:T(8,128)(2,1)}, bf16[9,1,128,1024]{3,2,1,0:T(8,128)(2,1)}, f32[9,1,...) while((s32[]{:T(128)}, bf16[32,1024]{1,0:T(8,128)(2,1)S(1)}, ...), condition=%wide.region_4.5_spmd, body=%wide.region_1.4_spmd.sunk | while | flops 555499648 | bytes 16911728 | solution.py:132
  77.7 22.5 %reduce-scatter.3.cloned.1.call-done = f32[32,1024]{1,0:T(8,128)} async-done(((f32[128,1024]{1,0:T(8,128)}), f32[32,1024]{1,0:T(8,128)}) %reduce-scatter.3.cloned.1.call-update) | async-done | bytes 131088 | tf_op jit(solution)/shard_map/while/body/eval_jaxpr/reduce_scatter | solution.py:31
  104.8 14.5 %all_gather.29 = bf16[128,1024]{1,0:T(8,128)(2,1)S(1)} all-gather(bf16[32,1024]{1,0:T(8,128)(2,1)S(1)} %get-tuple-element.782), channel_id=1, replica_groups=mesh['section'=4,'rep'=2,'tp'=4] {'tp'}, dimensions={0}, use_global_device_ids=true | all-gather | bytes 327680 | tf_op jit(solution)/shard_map/while/body/eval_jaxpr/all_gather | solution.py:23
  122.6 23.1 %reduce-scatter.3.cloned.1.call-done = f32[32,1024]{1,0:T(8,128)} async-done(((f32[128,1024]{1,0:T(8,128)}), f32[32,1024]{1,0:T(8,128)}) %reduce-scatter.3.cloned.1.call-update) | async-done | bytes 131088 | tf_op jit(solution)/shard_map/while/body/eval_jaxpr/reduce_scatter | solution.py:31
  150.5 14.5 %all_gather.29 = bf16[128,1024]{1,0:T(8,128)(2,1)S(1)} all-gather(bf16[32,1024]{1,0:T(8,128)(2,1)S(1)} %get-tuple-element.782), channel_id=1, replica_groups=mesh['section'=4,'rep'=2,'tp'=4] {'tp'}, dimensions={0}, use_global_device_ids=true | all-gather | bytes 327680 | tf_op jit(solution)/shard_map/while/body/eval_jaxpr/all_gather | solution.py:23
  168.2 23.2 %reduce-scatter.3.cloned.1.call-done = f32[32,1024]{1,0:T(8,128)} async-done(((f32[128,1024]{1,0:T(8,128)}), f32[32,1024]{1,0:T(8,128)}) %reduce-scatter.3.cloned.1.call-update) | async-done | bytes 131088 | tf_op jit(solution)/shard_map/while/body/eval_jaxpr/reduce_scatter | solution.py:31
  196.1 14.5 %all_gather.29 = bf16[128,1024]{1,0:T(8,128)(2,1)S(1)} all-gather(bf16[32,1024]{1,0:T(8,128)(2,1)S(1)} %get-tuple-element.782), channel_id=1, replica_groups=mesh['section'=4,'rep'=2,'tp'=4] {'tp'}, dimensions={0}, use_global_device_ids=true | all-gather | bytes 327680 | tf_op jit(solution)/shard_map/while/body/eval_jaxpr/all_gather | solution.py:23
  213.9 23.2 %reduce-scatter.3.cloned.1.call-done = f32[32,1024]{1,0:T(8,128)} async-done(((f32[128,1024]{1,0:T(8,128)}), f32[32,1024]{1,0:T(8,128)}) %reduce-scatter.3.cloned.1.call-update) | async-done | bytes 131088 | tf_op jit(solution)/shard_map/while/body/eval_jaxpr/reduce_scatter | solution.py:31
  241.8 14.5 %all_gather.29 = bf16[128,1024]{1,0:T(8,128)(2,1)S(1)} all-gather(bf16[32,1024]{1,0:T(8,128)(2,1)S(1)} %get-tuple-element.782), channel_id=1, replica_groups=mesh['section'=4,'rep'=2,'tp'=4] {'tp'}, dimensions={0}, use_global_device_ids=true | all-gather | bytes 327680 | tf_op jit(solution)/shard_map/while/body/eval_jaxpr/all_gather | solution.py:23
  259.6 23.2 %reduce-scatter.3.cloned.1.call-done = f32[32,1024]{1,0:T(8,128)} async-done(((f32[128,1024]{1,0:T(8,128)}), f32[32,1024]{1,0:T(8,128)}) %reduce-scatter.3.cloned.1.call-update) | async-done | bytes 131088 | tf_op jit(solution)/shard_map/while/body/eval_jaxpr/reduce_scatter | solution.py:31
  287.5 14.5 %all_gather.29 = bf16[128,1024]{1,0:T(8,128)(2,1)S(1)} all-gather(bf16[32,1024]{1,0:T(8,128)(2,1)S(1)} %get-tuple-element.782), channel_id=1, replica_groups=mesh['section'=4,'rep'=2,'tp'=4] {'tp'}, dimensions={0}, use_global_device_ids=true | all-gather | bytes 327680 | tf_op jit(solution)/shard_map/while/body/eval_jaxpr/all_gather | solution.py:23
  305.2 23.2 %reduce-scatter.3.cloned.1.call-done = f32[32,1024]{1,0:T(8,128)} async-done(((f32[128,1024]{1,0:T(8,128)}), f32[32,1024]{1,0:T(8,128)}) %reduce-scatter.3.cloned.1.call-update) | async-done | bytes 131088 | tf_op jit(solution)/shard_map/while/body/eval_jaxpr/reduce_scatter | solution.py:31
  333.2 14.5 %all_gather.29 = bf16[128,1024]{1,0:T(8,128)(2,1)S(1)} all-gather(bf16[32,1024]{1,0:T(8,128)(2,1)S(1)} %get-tuple-element.782), channel_id=1, replica_groups=mesh['section'=4,'rep'=2,'tp'=4] {'tp'}, dimensions={0}, use_global_device_ids=true | all-gather | bytes 327680 | tf_op jit(solution)/shard_map/while/body/eval_jaxpr/all_gather | solution.py:23
  350.9 23.1 %reduce-scatter.3.cloned.1.call-done = f32[32,1024]{1,0:T(8,128)} async-done(((f32[128,1024]{1,0:T(8,128)}), f32[32,1024]{1,0:T(8,128)}) %reduce-scatter.3.cloned.1.call-update) | async-done | bytes 131088 | tf_op jit(solution)/shard_map/while/body/eval_jaxpr/reduce_scatter | solution.py:31
  378.7 14.5 %all_gather.29 = bf16[128,1024]{1,0:T(8,128)(2,1)S(1)} all-gather(bf16[32,1024]{1,0:T(8,128)(2,1)S(1)} %get-tuple-element.782), channel_id=1, replica_groups=mesh['section'=4,'rep'=2,'tp'=4] {'tp'}, dimensions={0}, use_global_device_ids=true | all-gather | bytes 327680 | tf_op jit(solution)/shard_map/while/body/eval_jaxpr/all_gather | solution.py:23
  396.5 23.1 %reduce-scatter.3.cloned.1.call-done = f32[32,1024]{1,0:T(8,128)} async-done(((f32[128,1024]{1,0:T(8,128)}), f32[32,1024]{1,0:T(8,128)}) %reduce-scatter.3.cloned.1.call-update) | async-done | bytes 131088 | tf_op jit(solution)/shard_map/while/body/eval_jaxpr/reduce_scatter | solution.py:31
  424.3 14.5 %all_gather.29 = bf16[128,1024]{1,0:T(8,128)(2,1)S(1)} all-gather(bf16[32,1024]{1,0:T(8,128)(2,1)S(1)} %get-tuple-element.782), channel_id=1, replica_groups=mesh['section'=4,'rep'=2,'tp'=4] {'tp'}, dimensions={0}, use_global_device_ids=true | all-gather | bytes 327680 | tf_op jit(solution)/shard_map/while/body/eval_jaxpr/all_gather | solution.py:23
  442.1 23.1 %reduce-scatter.3.cloned.1.call-done = f32[32,1024]{1,0:T(8,128)} async-done(((f32[128,1024]{1,0:T(8,128)}), f32[32,1024]{1,0:T(8,128)}) %reduce-scatter.3.cloned.1.call-update) | async-done | bytes 131088 | tf_op jit(solution)/shard_map/while/body/eval_jaxpr/reduce_scatter | solution.py:31
  470.0 14.4 %all_gather.29 = bf16[128,1024]{1,0:T(8,128)(2,1)S(1)} all-gather(bf16[32,1024]{1,0:T(8,128)(2,1)S(1)} %get-tuple-element.782), channel_id=1, replica_groups=mesh['section'=4,'rep'=2,'tp'=4] {'tp'}, dimensions={0}, use_global_device_ids=true | all-gather | bytes 327680 | tf_op jit(solution)/shard_map/while/body/eval_jaxpr/all_gather | solution.py:23
  487.7 23.2 %reduce-scatter.3.cloned.1.call-done = f32[32,1024]{1,0:T(8,128)} async-done(((f32[128,1024]{1,0:T(8,128)}), f32[32,1024]{1,0:T(8,128)}) %reduce-scatter.3.cloned.1.call-update) | async-done | bytes 131088 | tf_op jit(solution)/shard_map/while/body/eval_jaxpr/reduce_scatter | solution.py:31
  515.6 14.5 %all_gather.29 = bf16[128,1024]{1,0:T(8,128)(2,1)S(1)} all-gather(bf16[32,1024]{1,0:T(8,128)(2,1)S(1)} %get-tuple-element.782), channel_id=1, replica_groups=mesh['section'=4,'rep'=2,'tp'=4] {'tp'}, dimensions={0}, use_global_device_ids=true | all-gather | bytes 327680 | tf_op jit(solution)/shard_map/while/body/eval_jaxpr/all_gather | solution.py:23
  533.4 23.2 %reduce-scatter.3.cloned.1.call-done = f32[32,1024]{1,0:T(8,128)} async-done(((f32[128,1024]{1,0:T(8,128)}), f32[32,1024]{1,0:T(8,128)}) %reduce-scatter.3.cloned.1.call-update) | async-done | bytes 131088 | tf_op jit(solution)/shard_map/while/body/eval_jaxpr/reduce_scatter | solution.py:31
  560.3 542.4 %while.43 = (s32[]{:T(128)}, bf16[32,1024]{1,0:T(8,128)(2,1)}, f32[1,2,1024,704]{2,3,1,0:T(8,128)}, f32[1,704,1024]{2,1,0:T(8,128)}, s32[]{:T(128)}, /*index=5*/...) while((s32[]{:T(128)}, bf16[32,1024]{1,0:T(8,128)(2,1)}, ...), condition=%wide.region_9.10_spmd.clone, body=%wide.region_5.9_spmd.clone.sunk | while | flops 1114185856 | bytes 33326708 | solution.py:168
  561.2 14.5 %all_gather.30 = bf16[128,1024]{1,0:T(8,128)(2,1)S(1)} all-gather(bf16[32,1024]{1,0:T(8,128)(2,1)S(1)} %fusion.66), channel_id=1, replica_groups=mesh['section'=4,'rep'=2,'tp'=4] {'tp'}, dimensions={0}, use_global_device_ids=true | all-gather | bytes 327680 | tf_op jit(solution)/shard_map/while/body/eval_jaxpr/all_gather | solution.py:23
  585.4 18.8 %reduce-scatter.5.cloned.1.call-done = f32[32,1024]{1,0:T(8,128)} async-done(((f32[128,1024]{1,0:T(8,128)}), f32[32,1024]{1,0:T(8,128)}) %reduce-scatter.5.cloned.1.call-update) | async-done | bytes 131088 | tf_op jit(solution)/shard_map/while/body/eval_jaxpr/reduce_scatter | solution.py:31
  611.7 14.5 %all_gather.30 = bf16[128,1024]{1,0:T(8,128)(2,1)S(1)} all-gather(bf16[32,1024]{1,0:T(8,128)(2,1)S(1)} %fusion.66), channel_id=1, replica_groups=mesh['section'=4,'rep'=2,'tp'=4] {'tp'}, dimensions={0}, use_global_device_ids=true | all-gather | bytes 327680 | tf_op jit(solution)/shard_map/while/body/eval_jaxpr/all_gather | solution.py:23
  637.8 14.6 %reduce-scatter.5.cloned.1.call-done = f32[32,1024]{1,0:T(8,128)} async-done(((f32[128,1024]{1,0:T(8,128)}), f32[32,1024]{1,0:T(8,128)}) %reduce-scatter.5.cloned.1.call-update) | async-done | bytes 131088 | tf_op jit(solution)/shard_map/while/body/eval_jaxpr/reduce_scatter | solution.py:31
  660.9 14.5 %all_gather.30 = bf16[128,1024]{1,0:T(8,128)(2,1)S(1)} all-gather(bf16[32,1024]{1,0:T(8,128)(2,1)S(1)} %fusion.66), channel_id=1, replica_groups=mesh['section'=4,'rep'=2,'tp'=4] {'tp'}, dimensions={0}, use_global_device_ids=true | all-gather | bytes 327680 | tf_op jit(solution)/shard_map/while/body/eval_jaxpr/all_gather | solution.py:23
  687.0 14.7 %reduce-scatter.5.cloned.1.call-done = f32[32,1024]{1,0:T(8,128)} async-done(((f32[128,1024]{1,0:T(8,128)}), f32[32,1024]{1,0:T(8,128)}) %reduce-scatter.5.cloned.1.call-update) | async-done | bytes 131088 | tf_op jit(solution)/shard_map/while/body/eval_jaxpr/reduce_scatter | solution.py:31
  710.2 14.5 %all_gather.30 = bf16[128,1024]{1,0:T(8,128)(2,1)S(1)} all-gather(bf16[32,1024]{1,0:T(8,128)(2,1)S(1)} %fusion.66), channel_id=1, replica_groups=mesh['section'=4,'rep'=2,'tp'=4] {'tp'}, dimensions={0}, use_global_device_ids=true | all-gather | bytes 327680 | tf_op jit(solution)/shard_map/while/body/eval_jaxpr/all_gather | solution.py:23
  736.2 14.7 %reduce-scatter.5.cloned.1.call-done = f32[32,1024]{1,0:T(8,128)} async-done(((f32[128,1024]{1,0:T(8,128)}), f32[32,1024]{1,0:T(8,128)}) %reduce-scatter.5.cloned.1.call-update) | async-done | bytes 131088 | tf_op jit(solution)/shard_map/while/body/eval_jaxpr/reduce_scatter | solution.py:31
  759.4 14.5 %all_gather.30 = bf16[128,1024]{1,0:T(8,128)(2,1)S(1)} all-gather(bf16[32,1024]{1,0:T(8,128)(2,1)S(1)} %fusion.66), channel_id=1, replica_groups=mesh['section'=4,'rep'=2,'tp'=4] {'tp'}, dimensions={0}, use_global_device_ids=true | all-gather | bytes 327680 | tf_op jit(solution)/shard_map/while/body/eval_jaxpr/all_gather | solution.py:23
  785.4 14.6 %reduce-scatter.5.cloned.1.call-done = f32[32,1024]{1,0:T(8,128)} async-done(((f32[128,1024]{1,0:T(8,128)}), f32[32,1024]{1,0:T(8,128)}) %reduce-scatter.5.cloned.1.call-update) | async-done | bytes 131088 | tf_op jit(solution)/shard_map/while/body/eval_jaxpr/reduce_scatter | solution.py:31
  808.6 14.5 %all_gather.30 = bf16[128,1024]{1,0:T(8,128)(2,1)S(1)} all-gather(bf16[32,1024]{1,0:T(8,128)(2,1)S(1)} %fusion.66), channel_id=1, replica_groups=mesh['section'=4,'rep'=2,'tp'=4] {'tp'}, dimensions={0}, use_global_device_ids=true | all-gather | bytes 327680 | tf_op jit(solution)/shard_map/while/body/eval_jaxpr/all_gather | solution.py:23
  834.6 14.6 %reduce-scatter.5.cloned.1.call-done = f32[32,1024]{1,0:T(8,128)} async-done(((f32[128,1024]{1,0:T(8,128)}), f32[32,1024]{1,0:T(8,128)}) %reduce-scatter.5.cloned.1.call-update) | async-done | bytes 131088 | tf_op jit(solution)/shard_map/while/body/eval_jaxpr/reduce_scatter | solution.py:31
  857.8 14.5 %all_gather.30 = bf16[128,1024]{1,0:T(8,128)(2,1)S(1)} all-gather(bf16[32,1024]{1,0:T(8,128)(2,1)S(1)} %fusion.66), channel_id=1, replica_groups=mesh['section'=4,'rep'=2,'tp'=4] {'tp'}, dimensions={0}, use_global_device_ids=true | all-gather | bytes 327680 | tf_op jit(solution)/shard_map/while/body/eval_jaxpr/all_gather | solution.py:23
  883.8 14.6 %reduce-scatter.5.cloned.1.call-done = f32[32,1024]{1,0:T(8,128)} async-done(((f32[128,1024]{1,0:T(8,128)}), f32[32,1024]{1,0:T(8,128)}) %reduce-scatter.5.cloned.1.call-update) | async-done | bytes 131088 | tf_op jit(solution)/shard_map/while/body/eval_jaxpr/reduce_scatter | solution.py:31
  906.9 14.5 %all_gather.30 = bf16[128,1024]{1,0:T(8,128)(2,1)S(1)} all-gather(bf16[32,1024]{1,0:T(8,128)(2,1)S(1)} %fusion.66), channel_id=1, replica_groups=mesh['section'=4,'rep'=2,'tp'=4] {'tp'}, dimensions={0}, use_global_device_ids=true | all-gather | bytes 327680 | tf_op jit(solution)/shard_map/while/body/eval_jaxpr/all_gather | solution.py:23
  932.9 14.7 %reduce-scatter.5.cloned.1.call-done = f32[32,1024]{1,0:T(8,128)} async-done(((f32[128,1024]{1,0:T(8,128)}), f32[32,1024]{1,0:T(8,128)}) %reduce-scatter.5.cloned.1.call-update) | async-done | bytes 131088 | tf_op jit(solution)/shard_map/while/body/eval_jaxpr/reduce_scatter | solution.py:31
  956.1 14.5 %all_gather.30 = bf16[128,1024]{1,0:T(8,128)(2,1)S(1)} all-gather(bf16[32,1024]{1,0:T(8,128)(2,1)S(1)} %fusion.66), channel_id=1, replica_groups=mesh['section'=4,'rep'=2,'tp'=4] {'tp'}, dimensions={0}, use_global_device_ids=true | all-gather | bytes 327680 | tf_op jit(solution)/shard_map/while/body/eval_jaxpr/all_gather | solution.py:23
  982.1 14.6 %reduce-scatter.5.cloned.1.call-done = f32[32,1024]{1,0:T(8,128)} async-done(((f32[128,1024]{1,0:T(8,128)}), f32[32,1024]{1,0:T(8,128)}) %reduce-scatter.5.cloned.1.call-update) | async-done | bytes 131088 | tf_op jit(solution)/shard_map/while/body/eval_jaxpr/reduce_scatter | solution.py:31
  1005.3 14.5 %all_gather.30 = bf16[128,1024]{1,0:T(8,128)(2,1)S(1)} all-gather(bf16[32,1024]{1,0:T(8,128)(2,1)S(1)} %fusion.66), channel_id=1, replica_groups=mesh['section'=4,'rep'=2,'tp'=4] {'tp'}, dimensions={0}, use_global_device_ids=true | all-gather | bytes 327680 | tf_op jit(solution)/shard_map/while/body/eval_jaxpr/all_gather | solution.py:23
  1031.3 14.6 %reduce-scatter.5.cloned.1.call-done = f32[32,1024]{1,0:T(8,128)} async-done(((f32[128,1024]{1,0:T(8,128)}), f32[32,1024]{1,0:T(8,128)}) %reduce-scatter.5.cloned.1.call-update) | async-done | bytes 131088 | tf_op jit(solution)/shard_map/while/body/eval_jaxpr/reduce_scatter | solution.py:31
  1054.4 14.5 %all_gather.30 = bf16[128,1024]{1,0:T(8,128)(2,1)S(1)} all-gather(bf16[32,1024]{1,0:T(8,128)(2,1)S(1)} %fusion.66), channel_id=1, replica_groups=mesh['section'=4,'rep'=2,'tp'=4] {'tp'}, dimensions={0}, use_global_device_ids=true | all-gather | bytes 327680 | tf_op jit(solution)/shard_map/while/body/eval_jaxpr/all_gather | solution.py:23
  1080.4 14.7 %reduce-scatter.5.cloned.1.call-done = f32[32,1024]{1,0:T(8,128)} async-done(((f32[128,1024]{1,0:T(8,128)}), f32[32,1024]{1,0:T(8,128)}) %reduce-scatter.5.cloned.1.call-update) | async-done | bytes 131088 | tf_op jit(solution)/shard_map/while/body/eval_jaxpr/reduce_scatter | solution.py:31
  1114.0 34.3 %all-gather.7.cloned.1.call-done = bf16[2,704,1024]{2,1,0:T(8,128)(2,1)} async-done(((bf16[1,704,1024]{2,1,0:T(8,128)(2,1)}), bf16[2,704,1024]{2,1,0:T(8,128)(2,1)}) %all-gather.7.cloned.1.call-update) | async-done | bytes 2883600 | tf_op jit(solution)/shard_map/all_gather | solution.py:173
  1160.5 64.4 %all-gather.5.cloned.1.call-done = bf16[2,2,1024,704]{2,3,1,0:T(8,128)(2,1)} async-done(((bf16[1,2,1024,704]{2,3,1,0:T(8,128)(2,1)}), bf16[2,2,1024,704]{2,3,1,0:T(8,128)(2,1)}) %all-gather.5.cloned.1.call-update) | async-done | bytes 5767184 | tf_op jit(solution)/shard_map/all_gather | solution.py:172
  (382 shorter events, 375.6 us)
Async XLA Ops:
  7.2 45.6 %all-reduce.2.cloned.1.call-start = ((), (), s32[]{:S(2)}) async-start(), calls=%async_computation.2 | async-start | bytes 1048576 | tf_op jit(solution)/shard_map/psum | solution.py:94
  58.9 41.3 %reduce-scatter.3.cloned.1.call-start = ((), (), s32[]{:S(2)}) async-start(), calls=%async_computation.5 | async-start | bytes 655360 | tf_op jit(solution)/shard_map/while/body/eval_jaxpr/reduce_scatter | solution.py:31
  101.0 2.2 collective-permute-start
  103.2 42.5 %reduce-scatter.3.cloned.1.call-start = ((), (), s32[]{:S(2)}) async-start(), calls=%async_computation.5 | async-start | bytes 655360 | tf_op jit(solution)/shard_map/while/body/eval_jaxpr/reduce_scatter | solution.py:31
  146.7 2.2 collective-permute-start
  148.9 42.6 %reduce-scatter.3.cloned.1.call-start = ((), (), s32[]{:S(2)}) async-start(), calls=%async_computation.5 | async-start | bytes 655360 | tf_op jit(solution)/shard_map/while/body/eval_jaxpr/reduce_scatter | solution.py:31
  192.4 2.2 collective-permute-start
  194.5 42.6 %reduce-scatter.3.cloned.1.call-start = ((), (), s32[]{:S(2)}) async-start(), calls=%async_computation.5 | async-start | bytes 655360 | tf_op jit(solution)/shard_map/while/body/eval_jaxpr/reduce_scatter | solution.py:31
  238.0 2.2 collective-permute-start
  240.2 42.6 %reduce-scatter.3.cloned.1.call-start = ((), (), s32[]{:S(2)}) async-start(), calls=%async_computation.5 | async-start | bytes 655360 | tf_op jit(solution)/shard_map/while/body/eval_jaxpr/reduce_scatter | solution.py:31
  283.7 2.2 collective-permute-start
  285.9 42.6 %reduce-scatter.3.cloned.1.call-start = ((), (), s32[]{:S(2)}) async-start(), calls=%async_computation.5 | async-start | bytes 655360 | tf_op jit(solution)/shard_map/while/body/eval_jaxpr/reduce_scatter | solution.py:31
  329.4 2.2 collective-permute-start
  331.6 42.4 %reduce-scatter.3.cloned.1.call-start = ((), (), s32[]{:S(2)}) async-start(), calls=%async_computation.5 | async-start | bytes 655360 | tf_op jit(solution)/shard_map/while/body/eval_jaxpr/reduce_scatter | solution.py:31
  374.9 2.2 collective-permute-start
  377.1 42.5 %reduce-scatter.3.cloned.1.call-start = ((), (), s32[]{:S(2)}) async-start(), calls=%async_computation.5 | async-start | bytes 655360 | tf_op jit(solution)/shard_map/while/body/eval_jaxpr/reduce_scatter | solution.py:31
  420.5 2.2 collective-permute-start
  422.7 42.5 %reduce-scatter.3.cloned.1.call-start = ((), (), s32[]{:S(2)}) async-start(), calls=%async_computation.5 | async-start | bytes 655360 | tf_op jit(solution)/shard_map/while/body/eval_jaxpr/reduce_scatter | solution.py:31
  422.7 18.2 %copy-start.7 = (bf16[1,1,704,1024]{3,2,1,0:T(8,128)(2,1)S(1)}, bf16[1,1,704,1024]{3,2,1,0:T(8,128)(2,1)}, u32[]{:S(2)}) copy-start(bf16[1,1,704,1024]{3,2,1,0:T(8,128)(2,1)} %get-tuple-element.843) | copy-start | bytes 4325380 | tf_op jit(solution)/shard_map/while
  466.2 2.2 collective-permute-start
  468.4 42.6 %reduce-scatter.3.cloned.1.call-start = ((), (), s32[]{:S(2)}) async-start(), calls=%async_computation.5 | async-start | bytes 655360 | tf_op jit(solution)/shard_map/while/body/eval_jaxpr/reduce_scatter | solution.py:31
  511.8 2.2 collective-permute-start
  514.0 42.6 %reduce-scatter.3.cloned.1.call-start = ((), (), s32[]{:S(2)}) async-start(), calls=%async_computation.5 | async-start | bytes 655360 | tf_op jit(solution)/shard_map/while/body/eval_jaxpr/reduce_scatter | solution.py:31
  557.5 2.2 collective-permute-start
  560.3 43.9 %reduce-scatter.5.cloned.1.call-start = ((), (), s32[]{:S(2)}) async-start(), calls=%async_computation.6 | async-start | bytes 655360 | tf_op jit(solution)/shard_map/while/body/eval_jaxpr/reduce_scatter | solution.py:31
  606.3 4.5 collective-permute-start.1
  610.8 41.6 %reduce-scatter.5.cloned.1.call-start = ((), (), s32[]{:S(2)}) async-start(), calls=%async_computation.6 | async-start | bytes 655360 | tf_op jit(solution)/shard_map/while/body/eval_jaxpr/reduce_scatter | solution.py:31
  654.6 5.5 collective-permute-start.1
  660.0 41.6 %reduce-scatter.5.cloned.1.call-start = ((), (), s32[]{:S(2)}) async-start(), calls=%async_computation.6 | async-start | bytes 655360 | tf_op jit(solution)/shard_map/while/body/eval_jaxpr/reduce_scatter | solution.py:31
  703.8 5.5 collective-permute-start.1
  709.3 41.6 %reduce-scatter.5.cloned.1.call-start = ((), (), s32[]{:S(2)}) async-start(), calls=%async_computation.6 | async-start | bytes 655360 | tf_op jit(solution)/shard_map/while/body/eval_jaxpr/reduce_scatter | solution.py:31
  753.0 5.5 collective-permute-start.1
  758.5 41.5 %reduce-scatter.5.cloned.1.call-start = ((), (), s32[]{:S(2)}) async-start(), calls=%async_computation.6 | async-start | bytes 655360 | tf_op jit(solution)/shard_map/while/body/eval_jaxpr/reduce_scatter | solution.py:31
  802.2 5.5 collective-permute-start.1
  807.7 41.6 %reduce-scatter.5.cloned.1.call-start = ((), (), s32[]{:S(2)}) async-start(), calls=%async_computation.6 | async-start | bytes 655360 | tf_op jit(solution)/shard_map/while/body/eval_jaxpr/reduce_scatter | solution.py:31
  851.4 5.5 collective-permute-start.1
  856.9 41.5 %reduce-scatter.5.cloned.1.call-start = ((), (), s32[]{:S(2)}) async-start(), calls=%async_computation.6 | async-start | bytes 655360 | tf_op jit(solution)/shard_map/while/body/eval_jaxpr/reduce_scatter | solution.py:31
  900.5 5.5 collective-permute-start.1
  906.0 41.6 %reduce-scatter.5.cloned.1.call-start = ((), (), s32[]{:S(2)}) async-start(), calls=%async_computation.6 | async-start | bytes 655360 | tf_op jit(solution)/shard_map/while/body/eval_jaxpr/reduce_scatter | solution.py:31
  949.7 5.5 collective-permute-start.1
  955.2 41.5 %reduce-scatter.5.cloned.1.call-start = ((), (), s32[]{:S(2)}) async-start(), calls=%async_computation.6 | async-start | bytes 655360 | tf_op jit(solution)/shard_map/while/body/eval_jaxpr/reduce_scatter | solution.py:31
  998.9 5.5 collective-permute-start.1
  1004.4 41.5 %reduce-scatter.5.cloned.1.call-start = ((), (), s32[]{:S(2)}) async-start(), calls=%async_computation.6 | async-start | bytes 655360 | tf_op jit(solution)/shard_map/while/body/eval_jaxpr/reduce_scatter | solution.py:31
  1048.0 5.5 collective-permute-start.1
  1053.5 41.6 %reduce-scatter.5.cloned.1.call-start = ((), (), s32[]{:S(2)}) async-start(), calls=%async_computation.6 | async-start | bytes 655360 | tf_op jit(solution)/shard_map/while/body/eval_jaxpr/reduce_scatter | solution.py:31
  1097.2 5.5 collective-permute-start.1
  1102.7 45.6 %all-gather.7.cloned.1.call-start = ((), (), s32[]{:S(2)}) async-start(), calls=%async_computation.4 | async-start | bytes 4325376 | tf_op jit(solution)/shard_map/all_gather | solution.py:173
  1106.6 118.3 %all-gather.5.cloned.1.call-start = ((), (), s32[]{:S(2)}) async-start(), calls=%async_computation.3 | async-start | bytes 8650752 | tf_op jit(solution)/shard_map/all_gather | solution.py:172
  (42 other events, 418.6 us)
Sparse Core Ops, SparseCore 0:
  16.6 36.1 all-reduce.1
  77.8 22.2 reduce-scatter.2
  122.8 22.9 reduce-scatter.2
  168.3 23.0 reduce-scatter.2
  214.0 23.0 reduce-scatter.2
  259.7 23.0 reduce-scatter.2
  305.3 23.0 reduce-scatter.2
  351.0 22.9 reduce-scatter.2
  396.6 22.9 reduce-scatter.2
  442.3 22.9 reduce-scatter.2
  487.8 23.0 reduce-scatter.2
  533.5 23.0 reduce-scatter.2
  581.1 22.9 reduce-scatter.4
  631.7 20.6 reduce-scatter.4
  680.9 20.6 reduce-scatter.4
  730.2 20.6 reduce-scatter.4
  779.4 20.6 reduce-scatter.4
  828.6 20.6 reduce-scatter.4
  877.7 20.5 reduce-scatter.4
  926.9 20.6 reduce-scatter.4
  976.1 20.6 reduce-scatter.4
  1025.2 20.6 reduce-scatter.4
  1074.4 20.6 reduce-scatter.4
  1106.7 41.5 all-gather.6
  1150.4 74.4 all-gather.4
where the time goes:
time: 1250 us
  waiting for transfers between devices  555 us (44%)
  blocking collectives  318 us (25%)
  matrix products  182 us (15%)
  other arithmetic  114 us (9%)
  local copies, waits for them, and re-layouts  36.4 us (3%)
  starting transfers between devices  28.7 us (2%)
  between operations  14.5 us (1%)
    reduce_scatter x22, waiting for transfers between devices, reduce_rows(): lax.psum_scatter(jnp.einsum(form, left, right, preferred_element_type=jnp...  419 us
    all_gather x22, blocking collectives, gather_rows(): return lax.all_gather(values, 'tp', axis=0, tiled=True)  318 us
    dot_general x11, matrix products, layer_backward(): jnp.einsum('td,tkf->kdf', normed, d_both, preferred_element_type=jnp.floa...  66.1 us
    all_gather x1, waiting for transfers between devices, shards(): lax.all_gather(new_pair[None], 'rep', axis=0, tiled=True)  64.4 us
    dot_general x11, matrix products, layer_backward(): jnp.einsum('tf,td->fd', hidden, grad_full, preferred_element_type=jnp.flo...  45 us
    psum x1, waiting for transfers between devices, shards(): start_rows = lax.psum(looked.astype(jnp.bfloat16), 'section')  36.3 us
    all_gather x1, waiting for transfers between devices, shards(): lax.all_gather(new_out[None], 'rep', axis=0, tiled=True)  34.3 us
    dot_general x22, matrix products, reduce_rows(): jnp.einsum(form, left, right, preferred_element_type=jnp.float32)  29 us
  transfers between devices with their start and end apart: 47, of which 36 were waited for; matrix products, arithmetic and copies ran while one was open for 11% of the time, Pallas kernels for 0%

commit v1 on v0

v1 whole, which is shorter than its diff:
```python
import functools

import jax
import jax.numpy as jnp
from jax import lax
from jax.experimental import pallas as pl
from jax.experimental.pallas import tpu as pltpu
from jax.sharding import PartitionSpec as P

EPS = 1e-05
INNER_LR = 0.001
OUTER_LR = 0.7
MOMENTUM = 0.9
MESH = pl.DeviceIdType.MESH
NT = (((1,), (1,)), ((), ()))


def scale_rows(values):
    return lax.rsqrt(jnp.mean(values * values, axis=-1, keepdims=True) + EPS)


def dot(left, right):
    return jnp.dot(left, right, preferred_element_type=jnp.float32)


def dot_nt(left, right):
    return lax.dot_general(left, right, NT, preferred_element_type=jnp.float32)


def relay(
    sections,
    peers,
    x0,
    seeds,
    pair,
    down,
    normed_out,
    hidden_out,
    d_gate_out,
    d_up_out,
    grad_out,
    x_full,
    grad_full,
    part,
    back_part,
    inbox,
    back_inbox,
    rows_out,
    back_rows_out,
    gate_store,
    up_store,
    x_recv,
    grad_recv,
    part_recv,
    back_recv,
    x_send,
    grad_send,
    part_send,
    back_send,
    x_first,
    grad_first,
):
    section = lax.axis_index("section")
    me = lax.axis_index("tp")
    batches, own, _ = x0.shape
    first = section == 0
    final = section == sections - 1
    later = section < sections - 1
    after = section > 0

    def rows_of(index):
        return pl.ds(pl.multiple_of(index * own, own), own)

    mine = rows_of(me)

    def wait(ref, sem):
        pltpu.make_async_copy(ref, ref, sem).wait()

    def send(source, target, send_sem, recv_sem, device):
        pltpu.make_async_remote_copy(
            src_ref=source,
            dst_ref=target,
            send_sem=send_sem,
            recv_sem=recv_sem,
            device_id=device,
            device_id_type=MESH,
        ).start()

    def around(offset):
        return lax.rem(me + offset, peers)

    barrier = pltpu.get_barrier_semaphore()
    for offset in range(1, peers):
        pl.semaphore_signal(
            barrier, inc=1, device_id={"tp": around(offset)}, device_id_type=MESH
        )

    @pl.when(later)
    def _():
        for offset in range(peers):
            pl.semaphore_signal(
                barrier,
                inc=1,
                device_id={"section": section + 1, "tp": around(offset)},
                device_id_type=MESH,
            )

    @pl.when(after)
    def _():
        for offset in range(peers):
            pl.semaphore_signal(
                barrier,
                inc=1,
                device_id={"section": section - 1, "tp": around(offset)},
                device_id_type=MESH,
            )

    @pl.when(later & after)
    def _():
        pl.semaphore_wait(barrier, 3 * peers - 1)

    @pl.when(jnp.logical_not(later & after))
    def _():
        pl.semaphore_wait(barrier, 2 * peers - 1)

    def feed(rows, full, send_sem, recv_sem):
        def step(micro, carry):
            for offset in range(1, peers):
                send(
                    rows.at[micro],
                    full.at[micro, mine],
                    send_sem.at[micro],
                    recv_sem.at[micro],
                    {"tp": around(offset)},
                )
            full[micro, mine, :] = rows[micro]
            return carry

        lax.fori_loop(0, batches, step, 0)

    @pl.when(first)
    def _():
        feed(x0, x_full, x_first, x_recv)

    @pl.when(final)
    def _():
        feed(seeds, grad_full, grad_first, grad_recv)

    def arrive(micro, full, recv_sem, alone):
        @pl.when(alone)
        def _():
            wait(full.at[micro, pl.ds(0, (peers - 1) * own)], recv_sem.at[micro])

        @pl.when(jnp.logical_not(alone))
        def _():
            wait(full.at[micro], recv_sem.at[micro])

    def scatter(micro, source, box, send_sem, recv_sem):
        for offset in range(1, peers):
            send(
                source.at[micro, rows_of(around(offset))],
                box.at[micro, offset - 1],
                send_sem.at[micro],
                recv_sem.at[micro],
                {"tp": around(offset)},
            )

    def collect(micro, source, box, recv_sem):
        wait(box.at[micro], recv_sem.at[micro])
        total = source[micro, mine, :].astype(jnp.float32)
        for slot in range(peers - 1):
            total += box[micro, slot].astype(jnp.float32)
        return total

    def pass_along(micro, rows, full, send_sem, recv_sem, step):
        for offset in range(peers):
            send(
                rows.at[micro],
                full.at[micro, mine],
                send_sem.at[micro],
                recv_sem.at[micro],
                {"section": section + step, "tp": around(offset)},
            )

    def forward(micro):
        arrive(micro, x_full, x_recv, first)
        xf = x_full[micro].astype(jnp.float32)
        normed = (xf * scale_rows(xf)).astype(jnp.bfloat16)
        normed_out[micro] = normed
        gate = dot(normed, pair[0])
        upper = dot(normed, pair[1])
        gate_store[micro] = gate
        up_store[micro] = upper
        hidden = (gate * jax.nn.sigmoid(gate) * upper).astype(jnp.bfloat16)
        hidden_out[micro] = hidden

        @pl.when(later)
        def _():
            part[micro] = dot(hidden, down[...]).astype(jnp.bfloat16)
            scatter(micro, part, inbox, part_send, part_recv)

    def forward_end(micro):
        total = collect(micro, part, inbox, part_recv)
        xf = x_full[micro, mine, :].astype(jnp.float32)
        rows_out[micro] = (xf + total).astype(jnp.bfloat16)
        pass_along(micro, rows_out, x_full, x_send, x_recv, 1)

    def backward(micro):
        arrive(micro, grad_full, grad_recv, final)
        grad = grad_full[micro]
        grad_out[micro] = grad
        d_hidden = dot_nt(grad, down[...])
        gate = gate_store[micro]
        sig = jax.nn.sigmoid(gate)
        d_gate = (d_hidden * up_store[micro] * sig * (1.0 + gate * (1.0 - sig))).astype(
            jnp.bfloat16
        )
        d_up = (d_hidden * (gate * sig)).astype(jnp.bfloat16)
        d_gate_out[micro] = d_gate
        d_up_out[micro] = d_up

        @pl.when(after)
        def _():
            back_part[micro] = (dot_nt(d_gate, pair[0]) + dot_nt(d_up, pair[1])).astype(
                jnp.bfloat16
            )
            scatter(micro, back_part, back_inbox, back_send, back_recv)

    def backward_end(micro):
        d_norm = collect(micro, back_part, back_inbox, back_recv)
        xf = x_full[micro, mine, :].astype(jnp.float32)
        rinv = scale_rows(xf)
        d_x = (
            grad_full[micro, mine, :].astype(jnp.float32)
            + rinv * d_norm
            - xf * (rinv * rinv * rinv) * jnp.mean(d_norm * xf, axis=-1, keepdims=True)
        )
        back_rows_out[micro] = d_x.astype(jnp.bfloat16)
        pass_along(micro, back_rows_out, grad_full, grad_send, grad_recv, -1)

    delay = 2 * (sections - 1 - section)

    def step(tick, carry):
        @pl.when(tick < batches)
        def _():
            forward(tick)

        @pl.when(later & (tick >= 1) & (tick <= batches))
        def _():
            forward_end(tick - 1)

        micro = tick - delay

        @pl.when((micro >= 0) & (micro < batches))
        def _():
            backward(micro)

        @pl.when(after & (micro >= 1) & (micro <= batches))
        def _():
            backward_end(micro - 1)

        return carry

    lax.fori_loop(0, batches + 2 * (sections - 1) + 1, step, 0)

    def drain(micro, carry):
        some = pl.ds(0, (peers - 1) * own)

        @pl.when(first)
        def _():
            wait(x_full.at[micro, some], x_first.at[micro])

        @pl.when(final)
        def _():
            wait(grad_full.at[micro, some], grad_first.at[micro])

        @pl.when(later)
        def _():
            wait(part.at[micro, some], part_send.at[micro])
            wait(x_full.at[micro], x_send.at[micro])

        @pl.when(after)
        def _():
            wait(back_part.at[micro, some], back_send.at[micro])
            wait(grad_full.at[micro], grad_send.at[micro])

        return carry

    lax.fori_loop(0, batches, drain, 0)


def run_relay(x0, seeds, pair, down):
    sections, peers = lax.axis_size("section"), lax.axis_size("tp")
    batches, own, width = x0.shape
    hidden = down.shape[0]
    rows = own * peers

    def of(*shape, kind=jnp.bfloat16):
        return pltpu.VMEM((batches,) + shape, kind)

    def out(columns):
        return jax.ShapeDtypeStruct((batches, rows, columns), jnp.bfloat16)

    vmem = pl.BlockSpec(memory_space=pltpu.VMEM)
    flops = 2 * batches * rows * width * hidden * 6
    return pl.pallas_call(
        functools.partial(relay, sections, peers),
        out_shape=(out(width), out(hidden), out(hidden), out(hidden), out(width)),
        in_specs=[vmem] * 4,
        out_specs=(vmem,) * 5,
        scratch_shapes=[
            of(rows, width),
            of(rows, width),
            of(rows, width),
            of(rows, width),
            of(peers - 1, own, width),
            of(peers - 1, own, width),
            of(own, width),
            of(own, width),
            of(rows, hidden, kind=jnp.float32),
            of(rows, hidden, kind=jnp.float32),
        ]
        + [pltpu.SemaphoreType.DMA((batches,))] * 10,
        compiler_params=pltpu.CompilerParams(
            collective_id=0, has_side_effects=True, vmem_limit_bytes=60 * 1024 * 1024
        ),
        cost_estimate=pl.CostEstimate(
            flops=flops, bytes_accessed=32 * 1024 * 1024, transcendentals=0
        ),
    )(x0, seeds, pair, down)


def shards(
    token_ids,
    embed,
    w_in,
    w_down,
    outer_in,
    outer_down,
    moment_in,
    moment_down,
    cotangent,
    fragment,
):
    sections = lax.axis_size("section")
    section = lax.axis_index("section")
    replicas = lax.axis_size("rep")
    ids = token_ids[0]
    batches, own_rows = ids.shape
    vocab_part, width = embed.shape
    local_ids = ids - section * vocab_part
    inside = (local_ids >= 0) & (local_ids < vocab_part)
    looked = jnp.take(embed, jnp.clip(local_ids, 0, vocab_part - 1), axis=0).astype(jnp.float32)
    looked = jnp.where(inside[:, :, None], looked, 0.0)
    start_rows = lax.psum(looked.astype(jnp.bfloat16), "section")
    pairs = w_in[0, 0]
    downs = w_down[0, 0]
    normed, hidden, d_gate, d_up, grad = run_relay(start_rows, cotangent[0], pairs, downs)

    def weight_grad(left, right):
        return jnp.einsum("bti,btj->ij", left, right, preferred_element_type=jnp.float32)

    def other(values):
        return lax.ppermute(
            values, "rep", [(source, (source + 1) % replicas) for source in range(replicas)]
        )

    def total(values):
        summed = values.astype(jnp.float32)
        passing = values
        for _ in range(replicas - 1):
            passing = other(passing)
            summed = summed + passing.astype(jnp.float32)
        return summed

    def inner(weights, grads):
        return (weights.astype(jnp.float32) - INNER_LR * grads).astype(jnp.bfloat16)

    flag = lax.dynamic_index_in_dim(fragment, section, 0, keepdims=False)
    chosen = flag == 1

    def update(weights, grads, outer, moment):
        new = inner(weights, grads)
        mean = outer - total(new) / replicas
        next_moment = MOMENTUM * moment + mean
        next_outer = outer - OUTER_LR * (mean + MOMENTUM * next_moment)
        return (
            jnp.where(chosen, next_outer.astype(jnp.bfloat16), new),
            jnp.where(chosen, next_outer, outer),
            jnp.where(chosen, next_moment, moment),
        )

    down_new, down_outer, down_moment = update(
        downs, weight_grad(hidden, grad), outer_down[0], moment_down[0]
    )
    gate_new, gate_outer, gate_moment = update(
        pairs[0], weight_grad(normed, d_gate), outer_in[0, 0], moment_in[0, 0]
    )
    up_new, up_outer, up_moment = update(
        pairs[1], weight_grad(normed, d_up), outer_in[0, 1], moment_in[0, 1]
    )
    return (
        jnp.stack([gate_new, up_new])[None, None],
        down_new[None, None],
        jnp.stack([gate_outer, up_outer])[None],
        down_outer[None],
        jnp.stack([gate_moment, up_moment])[None],
        down_moment[None],
    )


def solution(mesh):
    return jax.shard_map(
        shards,
        mesh=mesh,
        in_specs=(
            P("rep", None, "tp"),
            P("section", None),
            P("rep", "section", None, None, "tp"),
            P("rep", "section", "tp", None),
            P("section", None, None, "tp"),
            P("section", "tp", None),
            P("section", None, None, "tp"),
            P("section", "tp", None),
            P("rep", None, "tp", None),
            P(),
        ),
        out_specs=(
            P("rep", "section", None, None, "tp"),
            P("rep", "section", "tp", None),
            P("section", None, None, "tp"),
            P("section", "tp", None),
            P("section", None, None, "tp"),
            P("section", "tp", None),
        ),
        check_vma=False,
    )
```

time: 1250 us -> 544 us (0.44)
  waiting for transfers between devices: 555 us -> 93.1 us
  Pallas kernels: 0 us -> 381 us
  blocking collectives: 318 us -> 0 us
  matrix products: 182 us -> 12.3 us
  other arithmetic: 114 us -> 29.6 us
  local copies, waits for them, and re-layouts: 36.4 us -> 9.65 us
  starting transfers between devices: 28.7 us -> 3.6 us
    reduce_scatter x22 -> x0, waiting for transfers between devices: 419 us -> none  [reduce_rows(): lax.psum_scatter(jnp.einsum(form, left, right, preferred_element_type=jnp...]
    pallas_call x0 -> x1, Pallas kernels: none -> 381 us  [run_relay(): pl.pallas_call(functools.partial(relay, sections, peers), out_shape=(out(...]
    all_gather x22 -> x0, blocking collectives: 318 us -> none  [gather_rows(): return lax.all_gather(values, 'tp', axis=0, tiled=True)]
    dot_general x66 -> x3, matrix products: 182 us -> 12.3 us  [weight_grad(): jnp.einsum('bti,btj->ij', left, right, preferred_element_type=jnp.float32)]
    all_gather x2 -> x0, waiting for transfers between devices: 98.7 us -> none  [the longest x1 64.4 us: shards(): lax.all_gather(new_pair[None], 'rep', axis=0, tiled=True)]
    ppermute x22 -> x3, waiting for transfers between devices: 0.69 us -> 59.5 us  [other(): lax.ppermute(values, 'rep', [(source, (source + 1) % replicas) for source...]
    convert_element_type x24 -> x0, other arithmetic: 30.8 us -> none  [the longest x11 11.6 us: layer_backward(): return (d_x.astype(jnp.bfloat16), g_pair, g_down)]
    dynamic_update_slice x22 -> x0, other arithmetic: 26.6 us -> none  [the longest x11 17.6 us: forward_tick(): lax.dynamic_update_slice(x_store, current[None, None], (slot, zero + 0, z...]
  transfers between devices with their start and end apart: 47 -> 4, of which waited for: 36 -> 4; matrix products, arithmetic and copies ran while one was open for 11% -> 6% of each run, Pallas kernels for 0% -> 0%
where the time goes in v1:
time: 544 us
  Pallas kernels  381 us (70%)
  waiting for transfers between devices  93.1 us (17%)
  other arithmetic  29.6 us (5%)
  between operations  14.8 us (3%)
  matrix products  12.3 us (2%)
  local copies, waits for them, and re-layouts  9.65 us (2%)
    pallas_call x1, Pallas kernels, run_relay(): pl.pallas_call(functools.partial(relay, sections, peers), out_shape=(out(...  381 us
    ppermute x3, waiting for transfers between devices, other(): lax.ppermute(values, 'rep', [(source, (source + 1) % replicas) for source...  59.5 us
    psum x1, waiting for transfers between devices, shards(): start_rows = lax.psum(looked.astype(jnp.bfloat16), 'section')  33.5 us
    dot_general x3, matrix products, weight_grad(): jnp.einsum('bti,btj->ij', left, right, preferred_element_type=jnp.float32)  12.3 us
  transfers between devices with their start and end apart: 4, of which 4 were waited for; matrix products, arithmetic and copies ran while one was open for 6% of the time, Pallas kernels for 0%

profile of v1, /device:TPU:0, one launch (start us, length us, event | category | flops | bytes accessed | tf_op | source)
XLA Modules:
  0.0 543.9 jit_solution(12790107166535153946)
XLA Ops:
  7.2 0.0 all-reduce.2.cloned.1.call-start
  7.2 0.7 compare_select_fusion
  7.9 0.7 compare_and_fusion
  8.6 0.7 and_bitcast_fusion
  9.3 0.1 reshape.75
  9.4 0.0 copy-start.2
  9.4 6.2 %gather_fusion = bf16[256,1024]{1,0:T(8,128)(2,1)S(1)} fusion(bf16[4096,1024]{1,0:T(8,128)(2,1)} %param.11, s32[1024]{0:T(1024)S(1)} %pad_clamp_fusion), kind=kCustom, calls=%fused_computation | custom fusion | bytes 1049600 | tf_op jit(solution)/shard_map/jit(_take)/gather | solution.py:353
  15.6 1.1 select_convert_fusion
  16.6 0.0 all-reduce.2.cloned.1.call-update
  16.7 0.0 copy-done.2
  16.7 2.8 copy.16
  19.4 33.5 %all-reduce.2.cloned.1.call-done.x0 = bf16[8,32,1024]{2,1,0:T(8,128)(2,1)} async-done(((bf16[8,32,1024]{2,1,0:T(8,128)(2,1)}), bf16[8,32,1024]{2,1,0:T(8,128)(2,1)}) %all-reduce.2.cloned.1.call-update) | async-done | bytes 524304 | tf_op jit(solution)/shard_map/psum | solution.py:355
  53.0 380.9 %shard_map.145 = (bf16[8,128,1024]{2,1,0:T(8,128)(2,1)}, bf16[8,128,704]{2,1,0:T(8,128)(2,1)}, bf16[8,128,704]{2,1,0:T(8,128)(2,1)}, bf16[8,128,704]{2,1,0:T(8,128)(2,1)}, bf16[8,128,1024]{2,1,0:T(8,128)(2,1)}) custom-call(bf16[8,32,1024]{2,1,0:T(8,128)(2,1)} %all-reduce.2.cloned.1.call-done.x0, bf16[8,32,1024]{2,1,0:T(8,128)(2,1)} %bitcast.160, ...), custom_call_target="tpu_custom_call" | custom-call | flops 8858370048 | bytes 33554432 | tf_op jit(solution)/shard_map/pallas_call | solution.py:306
  433.9 0.0 copy-start.4
  433.9 0.0 copy-start.5
  433.9 5.0 fusion.1
  438.9 1.5 collective-permute-start
  440.4 0.0 copy-done.4
  440.4 0.0 copy-done.5
  440.4 0.0 copy-start.3
  440.4 2.9 fusion
  443.3 0.6 collective-permute-start.1
  443.8 0.0 copy-done.3
  443.8 0.6 dynamic_slice.4
  445.1 0.0 slice-start
  445.1 0.0 slice-start.1
  445.1 0.0 slice-start.2
  445.1 4.4 fusion.5
  449.5 1.5 collective-permute-start.2
  451.0 22.7 %collective-permute-done = bf16[1024,704]{0,1:T(8,128)(2,1)} collective-permute-done((bf16[1024,704]{0,1:T(8,128)(2,1)}, bf16[1024,704]{0,1:T(8,128)(2,1)}, u32[]{:S(2)}, u32[]{:S(2)}) %collective-permute-start) | collective-permute-done | bytes 1441824 | tf_op jit(solution)/shard_map/ppermute | solution.py:364
  473.7 30.9 %collective-permute-done.1 = bf16[1024,704]{0,1:T(8,128)(2,1)} collective-permute-done((bf16[1024,704]{0,1:T(8,128)(2,1)}, bf16[1024,704]{0,1:T(8,128)(2,1)}, u32[]{:S(2)}, u32[]{:S(2)}) %collective-permute-start.1) | collective-permute-done | bytes 1441824 | tf_op jit(solution)/shard_map/ppermute | solution.py:364
  504.6 0.0 slice-done
  504.6 0.0 slice-done.1
  504.6 0.0 slice-start.3
  504.6 7.8 %select_bitcast_fusion.2 = (bf16[1,1024,704]{1,2,0:T(8,128)(2,1)S(1)}, bf16[1,1024,704]{1,2,0:T(8,128)(2,1)S(1)}) fusion(bf16[1024,704]{0,1:T(8,128)(2,1)} %fusion.1, pred[]{:T(512)} %bitcast, f32[1,2,1024,704]{2,3,1,0:T(8,128)S(1)} %bitcast.154, bf16[1024,704]{0,1:T(8,128)(2,1)} %collective-permute-done, f32[1,2,1024,704]{2,3,1,0:T(8,128)} %param.14, ...), kind=kLoop, calls=%fused_computation.39 | loop fusion | flops 18743296 | bytes 20185088 | tf_op jit(solution)/shard_map/stack | solution.py:403
  512.4 1.8 maximum_bitcast_fusion.2
  514.3 0.0 slice-done.2
  514.3 0.0 slice-done.3
  514.3 4.9 fusion.11
  519.2 0.0 copy-start
  519.2 0.0 copy-start.1
  519.2 5.5 %maximum_bitcast_fusion = (f32[1,2,1024,704]{2,3,1,0:T(8,128)}, f32[1,2,1024,704]{2,3,1,0:T(8,128)}) fusion(f32[1,1024,704]{1,2,0:T(8,128)S(1)} %get-tuple-element.20, f32[1,1024,704]{1,2,0:T(8,128)S(1)} %get-tuple-element.17, f32[1,1024,704]{1,2,0:T(8,128)S(1)} %get-tuple-element.21, f32[1,1024,704]{1,2,0:T(8,128)S(1)} %get-tuple-element.16), kind=kLoop, calls=%fused_computation.1 | loop fusion | flops 2883584 | bytes 23068672 | tf_op jit(solution)/shard_map/broadcast_in_dim | solution.py:405
  524.6 6.0 %collective-permute-done.2 = bf16[704,1024]{1,0:T(8,128)(2,1)S(1)} collective-permute-done((bf16[704,1024]{1,0:T(8,128)(2,1)S(1)}, bf16[704,1024]{1,0:T(8,128)(2,1)S(1)}, u32[]{:S(2)}, u32[]{:S(2)}) %collective-permute-start.2) | collective-permute-done | bytes 1441824 | tf_op jit(solution)/shard_map/ppermute | solution.py:364
  530.6 0.0 copy-done
  530.6 0.0 copy-done.1
  530.6 2.4 select_bitcast_fusion
  533.0 4.0 fusion.3
  (3 shorter events, 0.0 us)
Async XLA Ops:
  7.2 45.8 %all-reduce.2.cloned.1.call-start = ((), (), s32[]{:S(2)}) async-start(), calls=%async_computation | async-start | bytes 1048576 | tf_op jit(solution)/shard_map/psum | solution.py:355
  9.4 7.3 %copy-start.2 = (bf16[1,1,2,1024,704]{3,4,2,1,0:T(8,128)(2,1)S(1)}, bf16[1,1,2,1024,704]{3,4,2,1,0:T(8,128)(2,1)}, u32[]{:S(2)}) copy-start(bf16[1,1,2,1024,704]{3,4,2,1,0:T(8,128)(2,1)} %param.12) | copy-start | bytes 8650756
  433.9 6.5 %copy-start.4 = (bf16[8,128,1024]{2,1,0:T(8,128)(2,1)S(1)}, bf16[8,128,1024]{2,1,0:T(8,128)(2,1)}, u32[]{:S(2)}) copy-start(bf16[8,128,1024]{2,1,0:T(8,128)(2,1)} %get-tuple-element.11) | copy-start | bytes 6291460
  433.9 6.5 %copy-start.5 = (bf16[8,128,704]{2,1,0:T(8,128)(2,1)S(1)}, bf16[8,128,704]{2,1,0:T(8,128)(2,1)}, u32[]{:S(2)}) copy-start(bf16[8,128,704]{2,1,0:T(8,128)(2,1)} %get-tuple-element.13) | copy-start | bytes 4325380
  438.9 34.8 %collective-permute-start = (bf16[1024,704]{0,1:T(8,128)(2,1)}, bf16[1024,704]{0,1:T(8,128)(2,1)}, u32[]{:S(2)}, u32[]{:S(2)}) collective-permute-start(bf16[1024,704]{0,1:T(8,128)(2,1)} %fusion.1), channel_id=1, source_target_pairs={{0,4},{4,0},{1,5},{5,1},{2,6},{6,2},{3,7},{7,3},{8,12},{12,8},{9,1... | collective-permute-start | bytes 4325384 | tf_op jit(solution)/shard_map/ppermute | solution.py:364
  440.4 3.4 copy-start.3
  443.3 61.3 %collective-permute-start.1 = (bf16[1024,704]{0,1:T(8,128)(2,1)}, bf16[1024,704]{0,1:T(8,128)(2,1)}, u32[]{:S(2)}, u32[]{:S(2)}) collective-permute-start(bf16[1024,704]{0,1:T(8,128)(2,1)} %fusion), channel_id=1, source_target_pairs={{0,4},{4,0},{1,5},{5,1},{2,6},{6,2},{3,7},{7,3},{8,12},{12,8},{9,1... | collective-permute-start | bytes 4325384 | tf_op jit(solution)/shard_map/ppermute | solution.py:364
  445.1 59.5 %slice-start = ((s8[5767168]{0:T(1024)(128)(4,1)}), s8[4194304]{0:T(1024)(128)(4,1)S(1)}, s32[]{:S(2)}) async-start(s8[5767168]{0:T(1024)(128)(4,1)} %bitcast.153), calls=%async_computation.1 | async-start | bytes 8388608
  445.1 59.5 %slice-start.1 = ((s8[5767168]{0:T(1024)(128)(4,1)}), s8[1572864]{0:T(1024)(128)(4,1)S(1)}, s32[]{:S(2)}) async-start(s8[5767168]{0:T(1024)(128)(4,1)} %bitcast.153), calls=%async_computation.2 | async-start | bytes 3145728
  445.1 69.2 %slice-start.2 = ((s8[5767168]{0:T(1024)(128)(4,1)}), s8[4194304]{0:T(1024)(128)(4,1)S(1)}, s32[]{:S(2)}) async-start(s8[5767168]{0:T(1024)(128)(4,1)} %bitcast.155), calls=%async_computation.3 | async-start | bytes 8388608
  449.5 81.1 %collective-permute-start.2 = (bf16[704,1024]{1,0:T(8,128)(2,1)S(1)}, bf16[704,1024]{1,0:T(8,128)(2,1)S(1)}, u32[]{:S(2)}, u32[]{:S(2)}) collective-permute-start(bf16[704,1024]{1,0:T(8,128)(2,1)S(1)} %fusion.5), channel_id=1, source_target_pairs={{0,4},{4,0},{1,5},{5,1},{2,6},{6,2},{3,7},{7,3},{8,12},{12,8},{9,1... | collective-permute-start | bytes 4325384 | tf_op jit(solution)/shard_map/ppermute | solution.py:364
  504.6 9.7 %slice-start.3 = ((s8[5767168]{0:T(1024)(128)(4,1)}), s8[1572864]{0:T(1024)(128)(4,1)S(1)}, s32[]{:S(2)}) async-start(s8[5767168]{0:T(1024)(128)(4,1)} %bitcast.155), calls=%async_computation.4 | async-start | bytes 3145728
  519.2 11.5 %copy-start = (f32[1,704,1024]{2,1,0:T(8,128)S(1)}, f32[1,704,1024]{2,1,0:T(8,128)}, u32[]{:S(2)}) copy-start(f32[1,704,1024]{2,1,0:T(8,128)} %param.17) | copy-start | bytes 8650756
  519.2 11.5 %copy-start.1 = (f32[1,704,1024]{2,1,0:T(8,128)S(1)}, f32[1,704,1024]{2,1,0:T(8,128)}, u32[]{:S(2)}) copy-start(f32[1,704,1024]{2,1,0:T(8,128)} %param.15) | copy-start | bytes 8650756
Sparse Core Ops, SparseCore 0:
  16.8 36.1 all-reduce.1
